TPU v7x, 32 devices: a whole 2x2x4 slice. The times are simulated.
32 devices in a mesh: row: 8 (over y, x, core), col: 4 (over z).
Axes of the slice: x: 2, y: 2, z: 4, core: 2. Of those that a mesh axis runs over, the one named last changes fastest.
Arguments:
- vectors: bfloat16 [32, 1024, 512], P('col', 'row'), may hold values from -6 to 6
- right_factors: bfloat16 [32, 32, 1024, 128], P('row', 'col'), may hold values from -0.1875 to 0.1875
- left_factors: bfloat16 [32, 32, 1024, 128], P('row', 'col'), may hold values from -0.125 to 0.125
- tile_ranks: int32 [32, 32], P('row', 'col'), may hold values from 16 to 128
- owner_map: int32 [32], replicated, may hold values from 0 to 31, as said below
Outputs:
- applied: bfloat16 [32, 1024, 512], P('row', 'col')
Inputs may be any that keep to these rules, and one draw needn't show every extreme that they name: owner_map is a permutation of 0 to 31; the 4 stored tile rows held by index i of row (stored rows i * 4 to i * 4 + 3) belong to 4 different indices of row of applied, i + c mod 8 for the same 4 offsets c at every i.
All inputs are finite; a program needn't handle non-finite values.
Results may differ from a plain program's by a relative error of at most 0.0066.
Values may be sent and summed in bfloat16 or wider, within the bound.
A program may use at most 128 MiB of HBM per device.

v0:
```python
import jax
import jax.numpy as jnp
from jax import lax
from jax.sharding import PartitionSpec as P


def masked_coeffs(products, tile_ranks, rank_width):
    columns = jnp.arange(rank_width, dtype=jnp.int32)
    kept_mask = columns[None, None, :] < tile_ranks[:, :, None]
    return jnp.where(kept_mask[:, :, :, None], products, 0.0).astype(jnp.bfloat16)


def build_buffer(payload, owner_map, cycle_size):
    held_rows = payload.shape[0]
    own_rows = lax.dynamic_slice_in_dim(owner_map, lax.axis_index("row") * held_rows, held_rows)
    target = own_rows // held_rows
    devices = jnp.arange(cycle_size, dtype=jnp.int32)
    matches = target[None, :] == devices[:, None]
    present = jnp.any(matches, axis=1)
    source_slot = jnp.sum(
        jnp.where(matches, jnp.arange(held_rows, dtype=jnp.int32)[None, :], 0), axis=1
    )
    picked = jnp.take(payload, source_slot, axis=0)
    return jnp.where(present[:, None, None], picked, jnp.zeros_like(picked))


def pick_rows(received, owner_map, held_rows):
    wanted = lax.axis_index("row") * held_rows + jnp.arange(held_rows, dtype=jnp.int32)
    matches = owner_map[None, :] == wanted[:, None]
    anchor = jnp.sum(
        jnp.where(matches, jnp.arange(owner_map.shape[0], dtype=jnp.int32)[None, :], 0), axis=1
    )
    return jnp.take(received, anchor // held_rows, axis=0)


def on_device(vectors, right_factors, left_factors, tile_ranks, owner_map):
    held_rows = right_factors.shape[0]
    rank_width = right_factors.shape[3]
    cycle_size = lax.axis_size("row")
    products = jnp.einsum(
        "ikbr,kbv->ikrv",
        right_factors,
        lax.all_gather(vectors, "row", axis=1, tiled=True),
        preferred_element_type=jnp.float32,
    )
    coeffs = masked_coeffs(products, tile_ranks, rank_width)
    partial_rows = jnp.einsum(
        "ikbr,ikrv->ibv", left_factors, coeffs, preferred_element_type=jnp.float32
    )
    summed = lax.psum_scatter(partial_rows, "col", scatter_dimension=1, tiled=True).astype(
        jnp.bfloat16
    )
    buffer = build_buffer(summed, owner_map, cycle_size)
    received = lax.all_to_all(buffer, "row", split_axis=0, concat_axis=0, tiled=True)
    applied = pick_rows(received, owner_map, held_rows)
    return applied


def solution(mesh):
    placed = (
        P("col", "row", None),
        P("row", "col", None, None),
        P("row", "col", None, None),
        P("row", "col"),
        P(),
    )
    return jax.shard_map(
        on_device, mesh=mesh, in_specs=placed, out_specs=P("row", "col", None), check_vma=False
    )
```

profile of v0, /device:TPU:0, one launch (start us, length us, event | category | flops | bytes accessed | tf_op | source)
XLA Modules:
  0.0 271.4 jit_solution(948302696471374495)
XLA Ops:
  6.5 0.0 all-gather.2.cloned.1.call-start
  6.5 0.7 all-gather.2.cloned.1.call-update
  7.3 0.0 reduce-scatter.2.cloned.1.call-start
  7.3 0.8 iota_compare_fusion
  8.1 58.2 %all-gather.2.cloned.1.call-done = bf16[8,1024,512]{2,1,0:T(8,128)(2,1)} async-done(((bf16[8,128,512]{2,1,0:T(8,128)(2,1)}), bf16[8,1024,512]{2,1,0:T(8,128)(2,1)}) %all-gather.2.cloned.1.call-update) | async-done | bytes 8388624 | tf_op jit(solution)/shard_map/all_gather | solution.py:43
  66.3 17.0 %fusion.7 = f32[4,1024,512]{1,2,0:T(8,128)} fusion(bf16[4,8,1024,128]{3,2,1,0:T(8,128)(2,1)} %param.7, pred[4,8,128]{2,1,0:T(8,128)(4,1)S(1)} %iota_compare_fusion, bf16[4,8,1024,128]{3,2,1,0:T(8,128)(2,1)} %param.6, bf16[8,1024,512]{2,1,0:T(8,128)(2,1)} %all-gather.2.cloned.1.call-done), kind=kOutput, calls=%fused_computation.9 | convolution fusion | flops 8594128896 | bytes 33558528 | tf_op jit(solution)/shard_map/ikbr,ikrv->ibv/dot_general | solution.py:47
  83.3 0.0 copy-start
  83.3 0.0 reduce-scatter.2.cloned.1.call-update
  83.3 0.6 copy-done
  83.9 0.1 and_select_fusion.1
  84.0 0.1 select_reduce_fusion
  84.1 0.1 fusion.14
  84.2 143.9 %reduce-scatter.2.cloned.1.call-done = f32[4,256,512]{1,2,0:T(8,128)} async-done(((f32[4,1024,512]{1,2,0:T(8,128)}), f32[4,256,512]{1,2,0:T(8,128)}) %reduce-scatter.2.cloned.1.call-update) | async-done | bytes 2097168 | tf_op jit(solution)/shard_map/reduce_scatter | solution.py:50
  228.1 1.7 convert_element_type.7
  229.8 0.7 gather_fusion
  230.5 1.6 select_select_fusion
  232.1 3.7 %all-to-all-start = ((bf16[8,256,512]{1,2,0:T(8,128)(2,1)}), bf16[8,256,512]{1,2,0:T(8,128)(2,1)S(1)}, u32[]{:S(2)}, u32[]{:S(2)}) async-start(bf16[8,256,512]{1,2,0:T(8,128)(2,1)} %select_select_fusion), calls=%async_computation.1 | async-start | bytes 4194304 | tf_op jit(solution)/shard_map/all_to_all | solution.py:54
  235.8 0.2 select_reduce_fusion.1
  236.0 26.4 %all-to-all-done = bf16[8,256,512]{1,2,0:T(8,128)(2,1)S(1)} async-done(((bf16[8,256,512]{1,2,0:T(8,128)(2,1)}), bf16[8,256,512]{1,2,0:T(8,128)(2,1)S(1)}, u32[]{:S(2)}, u32[]{:S(2)}) %all-to-all-start) | async-done | bytes 2097184 | tf_op jit(solution)/shard_map/all_to_all | solution.py:54
  262.4 0.6 gather_fusion.1
  263.0 0.2 broadcast_select_fusion
  263.2 1.3 copy.7
  (7 shorter events, 0.1 us)
Async XLA Ops:
  6.5 59.7 %all-gather.2.cloned.1.call-start = ((), (), s32[]{:S(2)}) async-start(), calls=%async_computation.2 | async-start | bytes 9437184 | tf_op jit(solution)/shard_map/all_gather | solution.py:43
  7.3 220.8 %reduce-scatter.2.cloned.1.call-start = ((), (), s32[]{:S(2)}) async-start(), calls=%async_computation.3 | async-start | bytes 10485760 | tf_op jit(solution)/shard_map/reduce_scatter | solution.py:50
  83.3 0.7 copy-start
  232.1 30.3 %all-to-all-start = ((bf16[8,256,512]{1,2,0:T(8,128)(2,1)}), bf16[8,256,512]{1,2,0:T(8,128)(2,1)S(1)}, u32[]{:S(2)}, u32[]{:S(2)}) async-start(bf16[8,256,512]{1,2,0:T(8,128)(2,1)} %select_select_fusion), calls=%async_computation.1 | async-start | bytes 4194304 | tf_op jit(solution)/shard_map/all_to_all | solution.py:54
Sparse Core Ops, SparseCore 0:
  9.2 56.9 all-gather.1
  83.4 144.6 reduce-scatter.1
where the time goes:
time: 272 us; the launch traced here: 271 us
  waiting for transfers between devices  229 us (84%)
  matrix products  17 us (6%)
  between operations  13.4 us (5%)
  other arithmetic  4.76 us (2%)
  starting transfers between devices  3.7 us (1%)
  local copies, waits for them, and re-layouts  3.24 us (1%)
    reduce_scatter x1, waiting for transfers between devices, on_device(): lax.psum_scatter(partial_rows, 'col', scatter_dimension=1, tiled=True)  144 us
    all_gather x1, waiting for transfers between devices, on_device(): lax.all_gather(vectors, 'row', axis=1, tiled=True)  58.2 us
    all_to_all x1, waiting for transfers between devices, on_device(): lax.all_to_all(buffer, 'row', split_axis=0, concat_axis=0, tiled=True)  26.4 us
    dot_general x1, matrix products, on_device(): jnp.einsum('ikbr,ikrv->ibv', left_factors, coeffs, preferred_element_type...  17 us
  transfers between devices with their start and end apart: 3, of which 3 were waited for; matrix products, arithmetic and copies ran while one was open for 0% of the time, Pallas kernels for 0%

commit v1 on v0

--- a/solution.py
+++ b/solution.py
@@ -37,12 +37,22 @@
     held_rows = right_factors.shape[0]
     rank_width = right_factors.shape[3]
     cycle_size = lax.axis_size("row")
-    products = jnp.einsum(
-        "ikbr,kbv->ikrv",
-        right_factors,
-        lax.all_gather(vectors, "row", axis=1, tiled=True),
-        preferred_element_type=jnp.float32,
-    )
+    size, index, width = (lax.axis_size("row"), lax.axis_index("row"), vectors.shape[1])
+    right = [(i, (i + 1) % size) for i in range(size)]
+    held, total = (vectors, None)
+    for lap in range(size):
+        coming = lax.ppermute(held, "row", right) if lap < size - 1 else None
+        update = jnp.einsum(
+            "ikbr,kbv->ikrv",
+            lax.dynamic_slice_in_dim(
+                right_factors, (index - lap) % size * width, held.shape[1], axis=2
+            ),
+            held,
+            preferred_element_type=jnp.float32,
+        )
+        total = update if total is None else total + update
+        held = coming
+    products = total
     coeffs = masked_coeffs(products, tile_ranks, rank_width)
     partial_rows = jnp.einsum(
         "ikbr,ikrv->ibv", left_factors, coeffs, preferred_element_type=jnp.float32

time: 272 us -> 330 us (1.21)
  matrix products: 17 us -> 60.9 us
  waiting for transfers between devices: 229 us -> 243 us
    ppermute x0 -> x7, waiting for transfers between devices: none -> 71.2 us  [on_device(): coming = lax.ppermute(held, 'row', right) if lap < size - 1 else None]
    all_gather x1 -> x0, waiting for transfers between devices: 58.2 us -> none  [on_device(): lax.all_gather(vectors, 'row', axis=1, tiled=True)]
    dot_general x0 -> x7, matrix products: none -> 34.5 us  [on_device(): jnp.einsum('ikbr,kbv->ikrv', lax.dynamic_slice_in_dim(right_factors, (ind...]
    dot_general x1, matrix products: 17 us -> 26.4 us  [on_device(): jnp.einsum('ikbr,ikrv->ibv', left_factors, coeffs, preferred_element_type...]
  transfers between devices with their start and end apart: 3 -> 9, of which waited for: 3 -> 9; matrix products, arithmetic and copies ran while one was open for 0% -> 11% of each run, Pallas kernels for 0% -> 0%
where the time goes in v1:
time: 330 us
  waiting for transfers between devices  243 us (74%)
  matrix products  60.9 us (18%)
  between operations  13.5 us (4%)
  other arithmetic  4.89 us (1%)
  starting transfers between devices  4.17 us (1%)
    reduce_scatter x1, waiting for transfers between devices, on_device(): lax.psum_scatter(partial_rows, 'col', scatter_dimension=1, tiled=True)  146 us
    ppermute x7, waiting for transfers between devices, on_device(): coming = lax.ppermute(held, 'row', right) if lap < size - 1 else None  71.2 us
    dot_general x7, matrix products, on_device(): jnp.einsum('ikbr,kbv->ikrv', lax.dynamic_slice_in_dim(right_factors, (ind...  34.5 us
    dot_general x1, matrix products, on_device(): jnp.einsum('ikbr,ikrv->ibv', left_factors, coeffs, preferred_element_type...  26.4 us
    all_to_all x1, waiting for transfers between devices, on_device(): lax.all_to_all(buffer, 'row', split_axis=0, concat_axis=0, tiled=True)  26.4 us
  transfers between devices with their start and end apart: 9, of which 9 were waited for; matrix products, arithmetic and copies ran while one was open for 11% of the time, Pallas kernels for 0%

profile of v1, /device:TPU:0, one launch (start us, length us, event | category | flops | bytes accessed | tf_op | source)
XLA Modules:
  0.0 330.1 jit_solution(16218522115521776971)
XLA Ops:
  6.5 0.0 reduce-scatter.2.cloned.1.call-start
  6.5 0.5 collective-permute-start
  7.0 15.6 %collective-permute-done = bf16[8,128,512]{2,1,0:T(8,128)(2,1)S(1)} collective-permute-done((bf16[8,128,512]{2,1,0:T(8,128)(2,1)}, bf16[8,128,512]{2,1,0:T(8,128)(2,1)S(1)}, u32[]{:S(2)}, u32[]{:S(2)}) %collective-permute-start) | collective-permute-done | bytes 1048608 | tf_op jit(solution)/shard_map/ppermute | solution.py:44
  22.6 0.0 collective-permute-start.1
  22.6 15.1 %collective-permute-done.1 = bf16[8,128,512]{2,1,0:T(8,128)(2,1)S(1)} collective-permute-done((bf16[8,128,512]{2,1,0:T(8,128)(2,1)S(1)}, bf16[8,128,512]{2,1,0:T(8,128)(2,1)S(1)}, u32[]{:S(2)}, u32[]{:S(2)}) %collective-permute-start.1) | collective-permute-done | bytes 1048608 | tf_op jit(solution)/shard_map/ppermute | solution.py:44
  37.7 0.0 collective-permute-start.2
  37.7 15.1 %collective-permute-done.2 = bf16[8,128,512]{2,1,0:T(8,128)(2,1)S(1)} collective-permute-done((bf16[8,128,512]{2,1,0:T(8,128)(2,1)S(1)}, bf16[8,128,512]{2,1,0:T(8,128)(2,1)S(1)}, u32[]{:S(2)}, u32[]{:S(2)}) %collective-permute-start.2) | collective-permute-done | bytes 1048608 | tf_op jit(solution)/shard_map/ppermute | solution.py:44
  52.8 0.0 copy-start.1
  52.8 0.0 collective-permute-start.3
  52.8 15.1 %collective-permute-done.3 = bf16[8,128,512]{2,1,0:T(8,128)(2,1)S(1)} collective-permute-done((bf16[8,128,512]{2,1,0:T(8,128)(2,1)S(1)}, bf16[8,128,512]{2,1,0:T(8,128)(2,1)S(1)}, u32[]{:S(2)}, u32[]{:S(2)}) %collective-permute-start.3) | collective-permute-done | bytes 1048608 | tf_op jit(solution)/shard_map/ppermute | solution.py:44
  68.0 0.0 copy-done.1
  68.0 0.0 collective-permute-start.4
  68.0 0.0 copy-start
  68.0 0.9 iota_compare_fusion
  68.9 6.2 %fusion.24 = f32[8,4,128,512]{2,3,0,1:T(8,128)} fusion(bf16[8,128,512]{2,1,0:T(8,128)(2,1)} %param.5, bf16[4,8,1024,128]{3,2,1,0:T(8,128)(2,1)} %param.6, s32[]{:T(128)S(6)} %select_n.144), kind=kOutput, calls=%fused_computation.23 | convolution fusion | flops 536870912 | bytes 10485764 | tf_op jit(solution)/shard_map/ikbr,kbv->ikrv/dot_general | solution.py:45
  75.1 8.1 %collective-permute-done.4 = bf16[8,128,512]{2,1,0:T(8,128)(2,1)} collective-permute-done((bf16[8,128,512]{2,1,0:T(8,128)(2,1)S(1)}, bf16[8,128,512]{2,1,0:T(8,128)(2,1)}, u32[]{:S(2)}, u32[]{:S(2)}) %collective-permute-start.4) | collective-permute-done | bytes 1048608 | tf_op jit(solution)/shard_map/ppermute | solution.py:44
  83.2 0.0 collective-permute-start.5
  83.2 0.0 copy-done
  83.2 4.5 %fusion.22 = f32[8,4,128,512]{2,3,0,1:T(8,128)} fusion(bf16[8,128,512]{2,1,0:T(8,128)(2,1)S(1)} %collective-permute-done, bf16[4,8,1024,128]{3,2,1,0:T(8,128)(2,1)S(1)} %copy-done, s32[]{:T(128)S(6)} %select_n.146), kind=kOutput, calls=%fused_computation.21 | convolution fusion | flops 536870912 | bytes 10485764 | tf_op jit(solution)/shard_map/ikbr,kbv->ikrv/dot_general | solution.py:45
  87.7 0.0 copy-start.2
  87.7 4.5 %fusion.20 = f32[8,4,128,512]{2,3,0,1:T(8,128)} fusion(bf16[8,128,512]{2,1,0:T(8,128)(2,1)S(1)} %collective-permute-done.1, bf16[4,8,1024,128]{3,2,1,0:T(8,128)(2,1)S(1)} %copy-done, s32[]{:T(128)S(6)} %select_n.148), kind=kOutput, calls=%fused_computation.19 | convolution fusion | flops 536870912 | bytes 10485764 | tf_op jit(solution)/shard_map/ikbr,kbv->ikrv/dot_general | solution.py:45
  92.2 0.0 copy-done.2
  92.2 4.5 %fusion.18 = f32[8,4,128,512]{2,3,0,1:T(8,128)} fusion(bf16[8,128,512]{2,1,0:T(8,128)(2,1)S(1)} %copy-done.2, bf16[4,8,1024,128]{3,2,1,0:T(8,128)(2,1)S(1)} %copy-done, s32[]{:T(128)S(6)} %select_n.150), kind=kOutput, calls=%fused_computation.17 | convolution fusion | flops 536870912 | bytes 10485764 | tf_op jit(solution)/shard_map/ikbr,kbv->ikrv/dot_general | solution.py:45
  96.7 1.8 collective-permute-done.5
  98.5 0.0 collective-permute-start.6
  98.5 4.5 %fusion.16 = f32[8,4,128,512]{2,3,0,1:T(8,128)} fusion(bf16[8,128,512]{2,1,0:T(8,128)(2,1)S(1)} %collective-permute-done.3, bf16[4,8,1024,128]{3,2,1,0:T(8,128)(2,1)S(1)} %copy-done, s32[]{:T(128)S(6)} %select_n.152), kind=kOutput, calls=%fused_computation.15 | convolution fusion | flops 536870912 | bytes 10485764 | tf_op jit(solution)/shard_map/ikbr,kbv->ikrv/dot_general | solution.py:45
  103.0 5.7 %fusion.14 = f32[8,4,128,512]{2,3,0,1:T(8,128)} fusion(bf16[8,128,512]{2,1,0:T(8,128)(2,1)} %collective-permute-done.4, bf16[4,8,1024,128]{3,2,1,0:T(8,128)(2,1)S(1)} %copy-done, s32[]{:T(128)S(6)} %select_n.154), kind=kOutput, calls=%fused_computation.13 | convolution fusion | flops 536870912 | bytes 10485764 | tf_op jit(solution)/shard_map/ikbr,kbv->ikrv/dot_general | solution.py:45
  108.8 4.5 %fusion.12 = f32[8,4,128,512]{2,3,0,1:T(8,128)} fusion(bf16[8,128,512]{2,1,0:T(8,128)(2,1)S(1)} %collective-permute-done.5, bf16[4,8,1024,128]{3,2,1,0:T(8,128)(2,1)S(1)} %copy-done, s32[]{:T(128)S(6)} %select_n.156), kind=kOutput, calls=%fused_computation.11 | convolution fusion | flops 536870912 | bytes 10485764 | tf_op jit(solution)/shard_map/ikbr,kbv->ikrv/dot_general | solution.py:45
  113.3 0.4 collective-permute-done.6
  113.7 26.4 %fusion.5 = f32[4,1024,512]{1,2,0:T(8,128)} fusion(bf16[4,8,1024,128]{3,2,1,0:T(8,128)(2,1)} %param.7, f32[8,4,128,512]{2,3,0,1:T(8,128)} %fusion.12, f32[8,4,128,512]{2,3,0,1:T(8,128)} %fusion.14, f32[8,4,128,512]{2,3,0,1:T(8,128)} %fusion.16, f32[8,4,128,512]{2,3,0,1:T(8,128)} %fusion.18, f32[8,4,128,512]{2,3,0,1:T(8,128)} %fusion.20, ...), kind=kOutput, calls=%fused_computation.7 | convolution fusion | flops 4850712576 | bytes 77598720 | tf_op jit(solution)/shard_map/ikbr,ikrv->ibv/dot_general | solution.py:57
  140.1 0.0 copy-start.3
  140.1 0.0 reduce-scatter.2.cloned.1.call-update
  140.1 0.6 copy-done.3
  140.7 0.1 and_select_fusion.1
  140.8 0.1 select_reduce_fusion
  140.9 0.1 fusion.35
  141.0 145.8 %reduce-scatter.2.cloned.1.call-done = f32[4,256,512]{1,2,0:T(8,128)} async-done(((f32[4,1024,512]{1,2,0:T(8,128)}), f32[4,256,512]{1,2,0:T(8,128)}) %reduce-scatter.2.cloned.1.call-update) | async-done | bytes 2097168 | tf_op jit(solution)/shard_map/reduce_scatter | solution.py:60
  286.9 1.7 convert_element_type.7
  288.5 0.7 gather_fusion
  289.2 1.6 select_select_fusion
  290.9 3.7 %all-to-all-start = ((bf16[8,256,512]{1,2,0:T(8,128)(2,1)}), bf16[8,256,512]{1,2,0:T(8,128)(2,1)S(1)}, u32[]{:S(2)}, u32[]{:S(2)}) async-start(bf16[8,256,512]{1,2,0:T(8,128)(2,1)} %select_select_fusion), calls=%async_computation.1 | async-start | bytes 4194304 | tf_op jit(solution)/shard_map/all_to_all | solution.py:64
  294.5 0.2 select_reduce_fusion.1
  294.8 26.4 %all-to-all-done = bf16[8,256,512]{1,2,0:T(8,128)(2,1)S(1)} async-done(((bf16[8,256,512]{1,2,0:T(8,128)(2,1)}), bf16[8,256,512]{1,2,0:T(8,128)(2,1)S(1)}, u32[]{:S(2)}, u32[]{:S(2)}) %all-to-all-start) | async-done | bytes 2097184 | tf_op jit(solution)/shard_map/all_to_all | solution.py:64
  321.1 0.6 gather_fusion.1
  321.8 0.2 broadcast_select_fusion
  321.9 1.3 copy.7
  (7 shorter events, 0.1 us)
Async XLA Ops:
  6.5 280.3 %reduce-scatter.2.cloned.1.call-start = ((), (), s32[]{:S(2)}) async-start(), calls=%async_computation.2 | async-start | bytes 10485760 | tf_op jit(solution)/shard_map/reduce_scatter | solution.py:60
  6.5 16.1 %collective-permute-start = (bf16[8,128,512]{2,1,0:T(8,128)(2,1)}, bf16[8,128,512]{2,1,0:T(8,128)(2,1)S(1)}, u32[]{:S(2)}, u32[]{:S(2)}) collective-permute-start(bf16[8,128,512]{2,1,0:T(8,128)(2,1)} %param.5), channel_id=1, source_target_pairs={{0,4},{4,8},{8,12},{12,16},{16,20},{20,24},{24,28},{28,0},{1,5},{5... | collective-permute-start | bytes 3145736 | tf_op jit(solution)/shard_map/ppermute | solution.py:44
  22.6 15.1 %collective-permute-start.1 = (bf16[8,128,512]{2,1,0:T(8,128)(2,1)S(1)}, bf16[8,128,512]{2,1,0:T(8,128)(2,1)S(1)}, u32[]{:S(2)}, u32[]{:S(2)}) collective-permute-start(bf16[8,128,512]{2,1,0:T(8,128)(2,1)S(1)} %collective-permute-done), channel_id=1, source_target_pairs={{0,4},{4,8},{8,12},{12,16},{16,20},{20,24},{24,28},{28,0},{1,5},{5... | collective-permute-start | bytes 3145736 | tf_op jit(solution)/shard_map/ppermute | solution.py:44
  37.7 15.1 %collective-permute-start.2 = (bf16[8,128,512]{2,1,0:T(8,128)(2,1)S(1)}, bf16[8,128,512]{2,1,0:T(8,128)(2,1)S(1)}, u32[]{:S(2)}, u32[]{:S(2)}) collective-permute-start(bf16[8,128,512]{2,1,0:T(8,128)(2,1)S(1)} %collective-permute-done.1), channel_id=1, source_target_pairs={{0,4},{4,8},{8,12},{12,16},{16,20},{20,24},{24,28},{28,0},{1,5},{5... | collective-permute-start | bytes 3145736 | tf_op jit(solution)/shard_map/ppermute | solution.py:44
  52.8 15.1 %copy-start.1 = (bf16[8,128,512]{2,1,0:T(8,128)(2,1)}, bf16[8,128,512]{2,1,0:T(8,128)(2,1)S(1)}, u32[]{:S(2)}) copy-start(bf16[8,128,512]{2,1,0:T(8,128)(2,1)S(1)} %collective-permute-done.2) | copy-start | bytes 3145732
  52.8 15.1 %collective-permute-start.3 = (bf16[8,128,512]{2,1,0:T(8,128)(2,1)S(1)}, bf16[8,128,512]{2,1,0:T(8,128)(2,1)S(1)}, u32[]{:S(2)}, u32[]{:S(2)}) collective-permute-start(bf16[8,128,512]{2,1,0:T(8,128)(2,1)S(1)} %collective-permute-done.2), channel_id=1, source_target_pairs={{0,4},{4,8},{8,12},{12,16},{16,20},{20,24},{24,28},{28,0},{1,5},{5... | collective-permute-start | bytes 3145736 | tf_op jit(solution)/shard_map/ppermute | solution.py:44
  68.0 15.2 %collective-permute-start.4 = (bf16[8,128,512]{2,1,0:T(8,128)(2,1)S(1)}, bf16[8,128,512]{2,1,0:T(8,128)(2,1)}, u32[]{:S(2)}, u32[]{:S(2)}) collective-permute-start(bf16[8,128,512]{2,1,0:T(8,128)(2,1)S(1)} %collective-permute-done.3), channel_id=1, source_target_pairs={{0,4},{4,8},{8,12},{12,16},{16,20},{20,24},{24,28},{28,0},{1,5},{5... | collective-permute-start | bytes 3145736 | tf_op jit(solution)/shard_map/ppermute | solution.py:44
  68.0 15.2 %copy-start = (bf16[4,8,1024,128]{3,2,1,0:T(8,128)(2,1)S(1)}, bf16[4,8,1024,128]{3,2,1,0:T(8,128)(2,1)}, u32[]{:S(2)}) copy-start(bf16[4,8,1024,128]{3,2,1,0:T(8,128)(2,1)} %param.6) | copy-start | bytes 25165828
  83.2 15.3 %collective-permute-start.5 = (bf16[8,128,512]{2,1,0:T(8,128)(2,1)}, bf16[8,128,512]{2,1,0:T(8,128)(2,1)S(1)}, u32[]{:S(2)}, u32[]{:S(2)}) collective-permute-start(bf16[8,128,512]{2,1,0:T(8,128)(2,1)} %collective-permute-done.4), channel_id=1, source_target_pairs={{0,4},{4,8},{8,12},{12,16},{16,20},{20,24},{24,28},{28,0},{1,5},{5... | collective-permute-start | bytes 3145736 | tf_op jit(solution)/shard_map/ppermute | solution.py:44
  87.7 4.5 %copy-start.2 = (bf16[8,128,512]{2,1,0:T(8,128)(2,1)S(1)}, bf16[8,128,512]{2,1,0:T(8,128)(2,1)}, u32[]{:S(2)}) copy-start(bf16[8,128,512]{2,1,0:T(8,128)(2,1)} %copy-done.1) | copy-start | bytes 3145732
  98.5 15.1 %collective-permute-start.6 = (bf16[8,128,512]{2,1,0:T(8,128)(2,1)S(1)}, bf16[8,128,512]{2,1,0:T(8,128)(2,1)S(1)}, u32[]{:S(2)}, u32[]{:S(2)}) collective-permute-start(bf16[8,128,512]{2,1,0:T(8,128)(2,1)S(1)} %collective-permute-done.5), channel_id=1, source_target_pairs={{0,4},{4,8},{8,12},{12,16},{16,20},{20,24},{24,28},{28,0},{1,5},{5... | collective-permute-start | bytes 3145736 | tf_op jit(solution)/shard_map/ppermute | solution.py:44
  140.1 0.7 copy-start.3
  290.9 30.3 %all-to-all-start = ((bf16[8,256,512]{1,2,0:T(8,128)(2,1)}), bf16[8,256,512]{1,2,0:T(8,128)(2,1)S(1)}, u32[]{:S(2)}, u32[]{:S(2)}) async-start(bf16[8,256,512]{1,2,0:T(8,128)(2,1)} %select_select_fusion), calls=%async_computation.1 | async-start | bytes 4194304 | tf_op jit(solution)/shard_map/all_to_all | solution.py:64
Sparse Core Ops, SparseCore 0:
  140.2 146.5 reduce-scatter.1
